TPU v7x, 32 devices: a whole 2x2x4 slice. The times are simulated.
32 devices in a mesh: snap: 8 (over z, x), bin: 4 (over y, core).
Axes of the slice: x: 2, y: 2, z: 4, core: 2. Of those that a mesh axis runs over, the one named last changes fastest.
Arguments:
- data: bfloat16 [256, 128, 1024], P(None, ('snap', 'bin')), may hold values from -6 to 6
- steering: bfloat16 [256, 1024, 2048], P(('snap', 'bin')), may hold values from -2 to 2
- start: float32 [256, 1024, 64], P(('snap', 'bin')), may hold values from -6 to 6
Outputs:
- projector: float32 [256, 1024, 1024], P(('snap', 'bin'))
- spectrum: float32 [2048], replicated
All inputs are finite; a program needn't handle non-finite values.
Results may differ from a plain program's by a relative error of at most 0.00042.
Values may be sent and summed in bfloat16 or wider, within the bound.
A program may use at most 128 MiB of HBM per device.

v0:
```python
import jax
import jax.numpy as jnp
from jax import lax
from jax.sharding import PartitionSpec as P

M = 1024
F = 256
ITERS = 3


def one_bin(snaps, steer, basis):
    covar = jnp.dot(snaps.T, snaps, preferred_element_type=jnp.float32) / snaps.shape[0]
    for step in range(ITERS):
        image = jnp.dot(covar, basis, precision=lax.Precision.HIGHEST)
        gram_mat = jnp.dot(image.T, image, precision=lax.Precision.HIGHEST)
        lower_factor = jnp.linalg.cholesky(gram_mat)
        basis = jax.scipy.linalg.solve_triangular(lower_factor, image.T, lower=True).T
    projector = jnp.dot(basis, basis.T, precision=lax.Precision.HIGHEST)
    basis_low = basis.astype(jnp.bfloat16)
    along = jnp.dot(basis_low.T, steer, preferred_element_type=jnp.float32)
    steer_wide = steer.astype(jnp.float32)
    energy = jnp.sum(steer_wide * steer_wide, axis=0)
    noise = energy - jnp.sum(along * along, axis=0)
    return (projector, noise)


def on_device(data, steering, start):
    owned = lax.all_to_all(
        lax.all_to_all(data, "snap", split_axis=0, concat_axis=1, tiled=True),
        "bin",
        split_axis=0,
        concat_axis=1,
        tiled=True,
    )
    projector, noise = lax.map(
        lambda items: one_bin(items[0], items[1], items[2]), (owned, steering, start)
    )
    overall = lax.psum(jnp.sum(noise, axis=0), ("snap", "bin"))
    spectrum = F * M / overall
    return (projector, spectrum)


def solution(mesh):
    return jax.shard_map(
        on_device,
        mesh=mesh,
        in_specs=(
            P(None, ("snap", "bin"), None),
            P(("snap", "bin"), None, None),
            P(("snap", "bin"), None, None),
        ),
        out_specs=(P(("snap", "bin"), None, None), P()),
        check_vma=False,
    )
```

profile of v0, /device:TPU:0, one launch (start us, length us, event | category | flops | bytes accessed | tf_op | source)
XLA Modules:
  0.0 705.3 jit_solution(12986566952320706374)
XLA Ops:
  0.6 55.5 %all_to_all.36 = bf16[256,4,1024]{2,1,0:T(4,128)(2,1)S(1)} all-to-all(bf16[256,4,1024]{2,1,0:T(4,128)(2,1)} %param.8), channel_id=1, replica_groups=mesh['snap'=8,'bin'=4] {'snap'}, dimensions={0} | all-to-all | bytes 4194304 | tf_op jit(solution)/shard_map/all_to_all | solution.py:29
  63.2 25.6 %all-to-all-done.1 = bf16[32,32,1024]{2,1,0:T(8,128)(2,1)S(1)} async-done(((bf16[32,32,1024]{2,1,0:T(8,128)(2,1)}), bf16[32,32,1024]{2,1,0:T(8,128)(2,1)S(1)}, u32[]{:S(2)}, u32[]{:S(2)}) %all-to-all-start.1) | async-done | bytes 2097184 | tf_op jit(solution)/shard_map/all_to_all | solution.py:28
  90.4 575.4 %while.12 = (s32[]{:T(128)}, f32[8,1024,1024]{2,1,0:T(8,128)}, f32[8,2048]{1,0:T(8,128)S(1)}, bf16[8,128,1024]{2,1,0:T(8,128)(2,1)}, f32[8,1024,64]{1,2,0:T(8,12...) while((s32[]{:T(128)}, f32[8,1024,1024]{2,1,0:T(8,128)}, f32[8,2048]{1,0:T(8,128)S(1)}, ...), condition=%wide.region_5.8_spmd, body=%wide.region_0.7_spmd.sunk | while | flops 4069959680 | bytes 51670652 | solution.py:35
  94.0 5.1 fusion.128
  99.6 5.8 cholesky.212
  112.1 6.4 fusion.134
  118.9 5.8 cholesky.213
  131.4 6.4 fusion.140
  138.2 5.8 cholesky.214
  145.5 4.9 custom-call.17
  150.9 5.0 bitcast_dynamic-update-slice_fusion.2
  166.0 5.1 fusion.128
  171.6 5.8 cholesky.212
  184.0 6.4 fusion.134
  190.9 5.8 cholesky.213
  198.0 4.9 custom-call.16
  203.3 6.4 fusion.140
  210.2 5.8 cholesky.214
  222.8 5.0 bitcast_dynamic-update-slice_fusion.2
  237.9 5.1 fusion.128
  243.5 5.8 cholesky.212
  250.6 4.9 custom-call.15
  255.9 6.4 fusion.134
  262.8 5.8 cholesky.213
  275.2 6.4 fusion.140
  282.1 5.8 cholesky.214
  289.4 4.9 custom-call.17
  294.7 5.0 bitcast_dynamic-update-slice_fusion.2
  309.8 5.1 fusion.128
  315.4 5.8 cholesky.212
  327.9 6.4 fusion.134
  334.7 5.8 cholesky.213
  347.2 6.4 fusion.140
  354.0 5.8 cholesky.214
  366.7 5.0 bitcast_dynamic-update-slice_fusion.2
  381.8 5.1 fusion.128
  387.4 5.8 cholesky.212
  399.8 6.4 fusion.134
  406.7 5.8 cholesky.213
  419.1 6.4 fusion.140
  426.0 5.8 cholesky.214
  438.6 5.0 bitcast_dynamic-update-slice_fusion.2
  453.7 5.1 fusion.128
  459.3 5.8 cholesky.212
  471.8 6.4 fusion.134
  478.6 5.8 cholesky.213
  491.1 6.4 fusion.140
  497.9 5.8 cholesky.214
  510.5 5.0 bitcast_dynamic-update-slice_fusion.2
  525.6 5.1 fusion.128
  531.2 5.8 cholesky.212
  543.7 6.4 fusion.134
  550.5 5.8 cholesky.213
  563.0 6.4 fusion.140
  569.8 5.8 cholesky.214
  582.5 5.0 bitcast_dynamic-update-slice_fusion.2
  597.6 5.1 fusion.128
  603.2 5.8 cholesky.212
  615.6 6.4 fusion.134
  622.5 5.8 cholesky.213
  634.9 6.4 fusion.140
  641.8 5.8 cholesky.214
  654.4 5.0 bitcast_dynamic-update-slice_fusion.2
  665.8 38.8 %psum.7 = f32[2048]{0:T(1024)S(1)} all-reduce(f32[2048]{0:T(1024)S(1)} %reduce_sum.27), channel_id=1, replica_groups=mesh['snap'=8,'bin'=4] {'snap','bin'}, use_global_device_ids=true, to_apply=%region_7.10 | all-reduce | flops 2048 | bytes 16384 | tf_op jit(solution)/shard_map/psum | solution.py:38
  (253 shorter events, 239.9 us)
Async XLA Ops:
  59.6 29.2 %all-to-all-start.1 = ((bf16[32,32,1024]{2,1,0:T(8,128)(2,1)}), bf16[32,32,1024]{2,1,0:T(8,128)(2,1)S(1)}, u32[]{:S(2)}, u32[]{:S(2)}) async-start(bf16[32,32,1024]{2,1,0:T(8,128)(2,1)} %copy.24), calls=%async_computation.1 | async-start | bytes 4194304 | tf_op jit(solution)/shard_map/all_to_all | solution.py:28
  92.1 1.9 copy-start
  164.0 1.9 copy-start
  236.0 1.9 copy-start
  307.9 1.9 copy-start
  379.9 1.9 copy-start
  451.8 1.9 copy-start
  523.7 1.9 copy-start
  595.6 1.9 copy-start
where the time goes:
time: 707 us; the launch traced here: 705 us
  other arithmetic  315 us (45%)
  matrix products  241 us (34%)
  blocking collectives  94.3 us (13%)
  waiting for transfers between devices  25.6 us (4%)
  local copies, waits for them, and re-layouts  23.7 us (3%)
    another operation x72, other arithmetic, one_bin(): lower_factor = jnp.linalg.cholesky(gram_mat)  157 us
    dot_general x24, matrix products, one_bin(): image = jnp.dot(covar, basis, precision=lax.Precision.HIGHEST)  143 us
    another operation x48, other arithmetic, one_bin(): jax.scipy.linalg.solve_triangular(lower_factor, image.T, lower=True)  132 us
    all_to_all x1, blocking collectives, on_device(): lax.all_to_all(data, 'snap', split_axis=0, concat_axis=1, tiled=True)  55.5 us
    dot_general x8, matrix products, one_bin(): projector = jnp.dot(basis, basis.T, precision=lax.Precision.HIGHEST)  40.4 us
    psum x1, blocking collectives, on_device(): overall = lax.psum(jnp.sum(noise, axis=0), ('snap', 'bin'))  38.8 us
    all_to_all x1, waiting for transfers between devices, on_device(): lax.all_to_all(lax.all_to_all(data, 'snap', split_axis=0, concat_axis=1,...  25.6 us
    reduce_sum x8, other arithmetic, one_bin(): energy = jnp.sum(steer_wide * steer_wide, axis=0)  24.6 us
  transfers between devices with their start and end apart: 1, of which 1 were waited for; matrix products, arithmetic and copies ran while one was open for 0% of the time, Pallas kernels for 0%

commit v1 on v0

v1 whole, which is shorter than its diff:
```python
import functools

import jax
import jax.numpy as jnp
from jax import lax
from jax.experimental import pallas as pl
from jax.experimental.pallas import tpu as pltpu

ITERS = 3
F32 = jnp.float32
BF16 = jnp.bfloat16
MESH = pl.DeviceIdType.MESH
VMEM_LIMIT = 64000 * 1024


def place(d, inner):
    return (d // inner, lax.rem(d, inner))


def greet_all(me, n, inner):
    barrier = pltpu.get_barrier_semaphore()

    def one(o, c):
        pl.semaphore_signal(
            barrier, inc=1, device_id=place(lax.rem(me + o, n), inner), device_id_type=MESH
        )
        return c

    lax.fori_loop(1, n, one, 0)
    pl.semaphore_wait(barrier, n - 1)


def exchange_kernel(n, inner, nb, data_ref, out_ref, send_sem, recv_sem, own_sem):
    me = lax.axis_index("snap") * inner + lax.axis_index("bin")
    own = pltpu.make_async_copy(data_ref.at[pl.ds(me * nb, nb)], out_ref.at[:, 0], own_sem)
    own.start()
    greet_all(me, n, inner)

    def copy(o):
        d = lax.rem(me + o, n)
        return pltpu.make_async_remote_copy(
            src_ref=data_ref.at[pl.ds(d * nb, nb)],
            dst_ref=out_ref.at[:, o],
            send_sem=send_sem.at[o],
            recv_sem=recv_sem.at[o],
            device_id=place(d, inner),
            device_id_type=MESH,
        )

    def start(o, c):
        copy(o).start()
        return c

    def finish(o, c):
        copy(o).wait()
        return c

    lax.fori_loop(1, n, start, 0)
    own.wait()
    lax.fori_loop(1, n, finish, 0)


def exchange(data, n, inner):
    bins, rows, width = data.shape
    nb = bins // n
    return pl.pallas_call(
        functools.partial(exchange_kernel, n, inner, nb),
        out_shape=jax.ShapeDtypeStruct((nb, n, rows, width), data.dtype),
        in_specs=[pl.BlockSpec(memory_space=pl.ANY)],
        out_specs=pl.BlockSpec(memory_space=pl.ANY),
        scratch_shapes=[
            pltpu.SemaphoreType.DMA((n,)),
            pltpu.SemaphoreType.DMA((n,)),
            pltpu.SemaphoreType.DMA,
        ],
        compiler_params=pltpu.CompilerParams(collective_id=0, has_side_effects=True),
        name="exchange",
    )(data)


def total_kernel(n, inner, scale, noise_ref, out_ref, held, send_sem, recv_sem):
    me = lax.axis_index("snap") * inner + lax.axis_index("bin")
    held[pl.ds(me, 1)] = noise_ref[...]
    greet_all(me, n, inner)

    def copy(o, slot):
        return pltpu.make_async_remote_copy(
            src_ref=noise_ref.at[0],
            dst_ref=held.at[slot],
            send_sem=send_sem.at[o],
            recv_sem=recv_sem.at[o],
            device_id=place(lax.rem(me + o, n), inner),
            device_id_type=MESH,
        )

    def start(o, c):
        copy(o, me).start()
        return c

    def finish(o, c):
        copy(o, lax.rem(me - o + n, n)).wait()
        return c

    lax.fori_loop(1, n, start, 0)
    lax.fori_loop(1, n, finish, 0)
    out_ref[...] = scale / jnp.sum(held[...], axis=0)


def total(noise, n, inner, scale):
    rows, width = noise.shape[1:]
    return pl.pallas_call(
        functools.partial(total_kernel, n, inner, scale),
        out_shape=jax.ShapeDtypeStruct((rows, width), F32),
        in_specs=[pl.BlockSpec(memory_space=pltpu.VMEM)],
        out_specs=pl.BlockSpec(memory_space=pltpu.VMEM),
        scratch_shapes=[
            pltpu.VMEM((n, rows, width), F32),
            pltpu.SemaphoreType.DMA((n,)),
            pltpu.SemaphoreType.DMA((n,)),
        ],
        compiler_params=pltpu.CompilerParams(collective_id=1, has_side_effects=True),
        name="total",
    )(noise)


def split(a):
    high = a.astype(BF16).astype(F32)
    rest = a - high
    mid = rest.astype(BF16).astype(F32)
    return high, mid, rest - mid


def stack(parts, axis):
    return jnp.concatenate(parts, axis=axis).astype(BF16)


def dot(a, b, ca, cb):
    return lax.dot_general(a, b, (((ca,), (cb,)), ((), ())), preferred_element_type=F32)


def fold_rows(p):
    r = p.shape[0] // 3
    return p[:r] + (p[r : 2 * r] + p[2 * r :])


def fold_lanes(p):
    c = p.shape[1] // 3
    return p[:, :c] + (p[:, c : 2 * c] + p[:, 2 * c :])


def inverse_factors(grams):
    size = grams[0].shape[0]
    eye = (
        lax.broadcasted_iota(jnp.int32, (size, size), 0)
        == lax.broadcasted_iota(jnp.int32, (size, size), 1)
    ).astype(F32)
    rest = [jnp.concatenate([g, eye], axis=1) for g in grams]
    wide = 2 * size
    sub = lax.broadcasted_iota(jnp.int32, (8, wide), 0)
    lane = lax.broadcasted_iota(jnp.int32, (8, size), 1)
    done = [[] for _ in grams]
    for t in range(size // 8):
        tiles = [a[8 * t : 8 * t + 8] for a in rest]
        cols = [
            [jnp.broadcast_to(a[:, 8 * t + j : 8 * t + j + 1], (8, wide)) for j in range(8)]
            for a in tiles
        ]
        invs = [jnp.zeros((8, wide), F32) for _ in tiles]
        for j in range(8):
            for i in range(len(tiles)):
                c = cols[i]
                inv = 1.0 / c[j][j : j + 1]
                below = jnp.where(sub > j, c[j], 0.0)
                tiles[i] = tiles[i] - below * (tiles[i][j : j + 1] * inv)
                for k in range(j + 1, 8):
                    c[k] = c[k] - below * (c[k][j : j + 1] * inv)
                invs[i] = jnp.where(sub == j, inv, invs[i])
        for i in range(len(tiles)):
            done[i].append(tiles[i] * jnp.sqrt(invs[i]))
            if 8 * t + 8 < size:
                scaled = (tiles[i] * invs[i])[:, :size]
                h, m, l = split(jnp.where(lane >= 8 * t + 8, scaled, 0.0))
                rh, rm, rl = split(tiles[i])
                rest[i] = rest[i] - dot(
                    stack([l, h, m, m, h, h], 0), stack([rh, rl, rm, rh, rm, rh], 0), 0, 0
                )
    return [jnp.concatenate(d, axis=0)[:, size:] for d in done]


def music_kernel(
    x_ref, start_ref, steer_ref, proj_ref, noise_ref, steer_v, out_v, s_v, v_v, in_sem, out_sem
):
    nb, kk, m = x_ref.shape
    width = start_ref.shape[2]
    g = steer_ref.shape[2]

    def load(b):
        return pltpu.make_async_copy(steer_ref.at[b], steer_v.at[b], in_sem.at[b])

    def put(b, slot):
        return pltpu.make_async_copy(out_v.at[slot], proj_ref.at[b], out_sem.at[slot])

    for b in range(nb):
        load(b).start()

    def prepare(b, c):
        x = x_ref[b]
        s_v[b] = stack(split(dot(x, x, 1, 1)), 1)
        y = dot(x, stack(split(start_ref[b]), 1), 1, 0)
        v_v[b] = fold_lanes(y).T
        return c

    lax.fori_loop(0, nb, prepare, 0)

    def step(it, c):
        last = it == ITERS - 1
        kept, grams = [], []
        for b in range(nb):
            v = v_v[b]
            vs = stack(split(v), 0)
            w = fold_rows(fold_lanes(dot(vs, s_v[b], 1, 0)))
            grams.append(fold_lanes(fold_rows(dot(stack(split(w), 0), vs, 1, 1))))
            kept.append(jnp.where(last, v, w * (1.0 / kk)))
        for b, factor in enumerate(inverse_factors(grams)):
            p = dot(stack(split(factor), 0), stack(split(kept[b]), 1), 1, 0)
            v_v[b] = fold_rows(fold_lanes(p))
        return c

    lax.fori_loop(0, ITERS, step, 0)
    noise_ref[...] = jnp.zeros_like(noise_ref)

    def finish(b, c):
        slot = lax.rem(b, 2)
        basis = fold_rows(dot(stack(split(v_v[b]), 0), x_ref[b], 1, 0))
        low = basis.astype(BF16)
        wide = low.astype(F32)
        tail = basis - wide
        left = stack([wide, tail, wide], 0)
        right = stack([wide, wide, tail], 0)

        @pl.when(b >= 2)
        def _():
            put(b - 2, slot).wait()

        step_rows = m // 4
        for r in range(0, m, step_rows):
            out_v[slot, r : r + step_rows] = dot(left[:, r : r + step_rows], right, 0, 0)
        put(b, slot).start()
        load(b).wait()
        step_lanes = g // 4
        for q in range(0, g, step_lanes):
            along = dot(low, steer_v[b, :, q : q + step_lanes], 1, 0)
            energy = jnp.zeros((8, step_lanes), F32)
            for r in range(0, m, 64):
                part = steer_v[b, r : r + 64, q : q + step_lanes].astype(F32)
                energy = energy + jnp.sum((part * part).reshape(8, 8, step_lanes), axis=0)
            noise_ref[0, :, q : q + step_lanes] += jnp.sum(energy, axis=0, keepdims=True) - jnp.sum(
                along * along, axis=0, keepdims=True
            )
        return c

    lax.fori_loop(0, nb, finish, 0)
    for b in range(max(nb - 2, 0), nb):
        put(b, b % 2).wait()


def music(x, start, steering):
    nb, kk, m = x.shape
    width = start.shape[2]
    g = steering.shape[2]
    return pl.pallas_call(
        music_kernel,
        out_shape=(
            jax.ShapeDtypeStruct((nb, m, m), F32),
            jax.ShapeDtypeStruct((1, 1, g), F32),
        ),
        in_specs=[
            pl.BlockSpec(memory_space=pltpu.VMEM),
            pl.BlockSpec(memory_space=pltpu.VMEM),
            pl.BlockSpec(memory_space=pl.ANY),
        ],
        out_specs=(
            pl.BlockSpec(memory_space=pl.ANY),
            pl.BlockSpec(memory_space=pltpu.VMEM),
        ),
        scratch_shapes=[
            pltpu.VMEM((nb, m, g), BF16),
            pltpu.VMEM((2, m, m), F32),
            pltpu.VMEM((nb, kk, 3 * kk), BF16),
            pltpu.VMEM((nb, width, kk), F32),
            pltpu.SemaphoreType.DMA((nb,)),
            pltpu.SemaphoreType.DMA((2,)),
        ],
        compiler_params=pltpu.CompilerParams(vmem_limit_bytes=VMEM_LIMIT),
        name="music",
    )(x, start, steering)


def on_device(n, inner, data, steering, start):
    bins, rows, m = data.shape
    owned = exchange(data, n, inner)
    owned = owned.reshape(owned.shape[0], n * rows, m)
    projector, noise = music(owned, start, steering)
    spectrum = total(noise, n, inner, float(bins * m))
    return (projector, spectrum.reshape(-1))


def solution(mesh):
    P = jax.sharding.PartitionSpec
    inner = mesh.shape["bin"]
    n = mesh.shape["snap"] * inner
    both = ("snap", "bin")
    return jax.shard_map(
        functools.partial(on_device, n, inner),
        mesh=mesh,
        in_specs=(P(None, both, None), P(both, None, None), P(both, None, None)),
        out_specs=(P(both, None, None), P()),
        check_vma=False,
    )
```

time: 707 us -> 118 us (0.17)
  other arithmetic: 315 us -> 0 us
  matrix products: 241 us -> 0 us
  Pallas kernels: 0 us -> 109 us
  blocking collectives: 94.3 us -> 0 us
  waiting for transfers between devices: 25.6 us -> 0 us
  local copies, waits for them, and re-layouts: 23.7 us -> 8.11 us
    another operation x120 -> x0, other arithmetic: 290 us -> none  [the longest x72 157 us: one_bin(): lower_factor = jnp.linalg.cholesky(gram_mat)]
    dot_general x72 -> x0, matrix products: 231 us -> none  [the longest x24 143 us: one_bin(): image = jnp.dot(covar, basis, precision=lax.Precision.HIGHEST)]
    pallas_call x0 -> x3, Pallas kernels: none -> 109 us  [the longest x1 45 us: exchange(): pl.pallas_call(functools.partial(exchange_kernel, n, inner, nb), out_shap...]
    all_to_all x1 -> x0, blocking collectives: 55.5 us -> none  [on_device(): lax.all_to_all(data, 'snap', split_axis=0, concat_axis=1, tiled=True)]
    psum x1 -> x0, blocking collectives: 38.8 us -> none  [on_device(): overall = lax.psum(jnp.sum(noise, axis=0), ('snap', 'bin'))]
    all_to_all x1 -> x0, waiting for transfers between devices: 25.6 us -> none  [on_device(): lax.all_to_all(lax.all_to_all(data, 'snap', split_axis=0, concat_axis=1,...]
    reduce_sum x9 -> x0, other arithmetic: 24.6 us -> none  [the longest x8 24.6 us: one_bin(): energy = jnp.sum(steer_wide * steer_wide, axis=0)]
    while x16 -> x0, local copies, waits for them, and re-layouts: 15.4 us -> none
  transfers between devices with their start and end apart: 1 -> 0, of which waited for: 1 -> 0; matrix products, arithmetic and copies ran while one was open for 0% -> 0% of each run, Pallas kernels for 0% -> 0%
where the time goes in v1:
time: 118 us; the launch traced here: 117 us
  Pallas kernels  109 us (92%)
  local copies, waits for them, and re-layouts  8.11 us (7%)
    pallas_call x1, Pallas kernels, exchange(): pl.pallas_call(functools.partial(exchange_kernel, n, inner, nb), out_shap...  45 us
    pallas_call x1, Pallas kernels, music(): pl.pallas_call(music_kernel, out_shape=(jax.ShapeDtypeStruct((nb, m, m),...  40.6 us
    pallas_call x1, Pallas kernels, total(): pl.pallas_call(functools.partial(total_kernel, n, inner, scale), out_shap...  23.1 us
    reshape x1, local copies, waits for them, and re-layouts, on_device(): owned = owned.reshape(owned.shape[0], n * rows, m)  4.11 us
    unnamed x4, local copies, waits for them, and re-layouts  4 us

profile of v1, /device:TPU:0, one launch (start us, length us, event | category | flops | bytes accessed | tf_op | source)
XLA Modules:
  0.0 117.5 jit_solution(1843566855357787554)
XLA Ops:
  0.6 45.0 %exchange.1 = bf16[8,32,4,1024]{3,2,1,0:T(4,128)(2,1)} custom-call(bf16[256,4,1024]{2,1,0:T(4,128)(2,1)} %data_ref.1), custom_call_target="tpu_custom_call" | custom-call | tf_op jit(solution)/shard_map/exchange/pallas_call | solution.py:66
  45.7 0.0 copy-start
  45.7 4.1 %reshape.10.x_ref = bf16[8,128,1024]{2,1,0:T(8,128)(2,1)} reshape(bf16[8,32,4,1024]{3,2,1,0:T(4,128)(2,1)} %exchange.1) | data formatting | bytes 4194304 | tf_op jit(solution)/shard_map/reshape | solution.py:302
  49.8 0.0 copy-done
  49.8 2.7 %copy.5.start_ref = f32[8,1024,64]{2,1,0:T(8,128)} copy(f32[8,1024,64]{1,2,0:T(8,128)S(1)} %copy-done) | data formatting | bytes 4194304 | tf_op args[2]
  52.5 40.6 %music.1 = (f32[8,1024,1024]{2,1,0:T(8,128)}, f32[1,1,2048]{2,1,0:T(1,128)}) custom-call(bf16[8,128,1024]{2,1,0:T(8,128)(2,1)} %reshape.10.x_ref, f32[8,1024,64]{2,1,0:T(8,128)} %copy.5.start_ref, bf16[8,1024,2048]{2,1,0:T(8,128)(2,1)} %steer_ref.1), custom_call_target="tpu_custom_call" | custom-call | tf_op jit(solution)/shard_map/music/pallas_call | solution.py:271
  93.0 23.1 %total.1 = f32[1,2048]{1,0:T(1,128)} custom-call(f32[1,1,2048]{2,1,0:T(1,128)} %get-tuple-element.5.noise_ref), custom_call_target="tpu_custom_call" | custom-call | tf_op jit(solution)/shard_map/total/pallas_call | solution.py:111
  116.2 1.3 %copy.7 = f32[2048]{0:T(1024)} copy(f32[2048]{0:T(1024)} %bitcast.1) | data formatting | bytes 16384
Async XLA Ops:
  45.7 4.1 %copy-start = (f32[8,1024,64]{1,2,0:T(8,128)S(1)}, f32[8,1024,64]{1,2,0:T(8,128)}, u32[]{:S(2)}) copy-start(f32[8,1024,64]{1,2,0:T(8,128)} %param.5) | copy-start | bytes 6291460
